TPU v7x, 128 devices: a whole 4x4x4 slice. The times are simulated.
128 devices in a mesh: py: 8 (over z, x_hi), px: 4 (over y_hi, core), pz: 4 (over y_lo, x_lo).
Axes of the slice: x: 4 (x_hi: 2, x_lo: 2; x = x_hi * 2 + x_lo), y: 4 (y_hi: 2, y_lo: 2; y = y_hi * 2 + y_lo), z: 4, core: 2. Of those that a mesh axis runs over, the one named last changes fastest.
Arguments:
- initial_density: float32 [32, 256, 384, 128], P('py', 'px', 'pz'), may hold values from 0.2 to 1.8
- inverse_limit: float32 [32, 256, 384, 128], P('py', 'px', 'pz'), may hold values from 0.5 to 2
Outputs:
- temperature_end: float32 [32, 256, 384, 128], P('py', 'px', 'pz')
All inputs are finite; a program needn't handle non-finite values.
Results may differ from a plain program's by a relative error of at most 0.00002.
Values sent between devices are 32-bit elements; how exact they have to be, the bound alone decides.
A program may use at most 384 MiB of HBM per device.

v0:
```python
import jax
import jax.numpy as jnp
from jax import lax
from jax.sharding import PartitionSpec as P

STEPS = 3


def extended(x, sides, width):
    edges = {}
    for axis, dim in sides:
        peers, length = (lax.axis_size(axis), x.shape[dim])
        up = [(i, (i + 1) % peers) for i in range(peers - 1)]
        last = lax.slice_in_dim(x, length - width, length, axis=dim)
        leading = lax.slice_in_dim(x, 0, width, axis=dim)
        edges[dim] = (
            lax.ppermute(last, axis, up),
            lax.ppermute(leading, axis, [(b, a) for a, b in up]),
        )
    done = []
    for _, dim in sides:
        low, high = edges[dim]
        around = [(width, width) if d in done else (0, 0) for d in range(x.ndim)]
        x = jnp.concatenate([jnp.pad(low, around), x, jnp.pad(high, around)], axis=dim)
        done.append(dim)
    return x


def inner_cells(values, dims):
    for dim in dims:
        values = lax.slice_in_dim(values, 1, values.shape[dim] - 1, axis=dim)
    return values


def boundary_cells(values, dim, start, dims):
    remaining_parts = [other for other in dims if other != dim]
    values = inner_cells(values, remaining_parts)
    return lax.slice_in_dim(values, start, start + values.shape[dim] - 2, axis=dim)


def advance_population(haloed_population, inverse_limit):
    middle = inner_cells(haloed_population, (0, 1, 2))
    lower = [boundary_cells(haloed_population, dim, 0, (0, 1, 2)) for dim in (0, 1, 2)]
    upper = [boundary_cells(haloed_population, dim, 2, (0, 1, 2)) for dim in (0, 1, 2)]
    spread = lower[0] + upper[0] + lower[1] + upper[1] + lower[2] + upper[2] - 6.0 * middle
    return middle + 0.1 * spread + 0.2 * middle * (1.0 - middle * inverse_limit)


def local(initial_density, inverse_limit):
    for step in range(STEPS):
        haloed_population = extended(initial_density, (("py", 0), ("px", 1), ("pz", 2)), 1)
        initial_density = advance_population(haloed_population, inverse_limit)
    return initial_density


def solution(mesh):
    in_specs = (P("py", "px", "pz", None), P("py", "px", "pz", None))
    out_specs = P("py", "px", "pz", None)
    return jax.shard_map(local, mesh=mesh, in_specs=in_specs, out_specs=out_specs, check_vma=False)
```

profile of v0, /device:TPU:7, one launch (start us, length us, event | category | flops | bytes accessed | tf_op | source)
XLA Modules:
  0.0 579.7 jit_solution(3034799448884535832)
XLA Ops:
  0.0 5.0 fusion.41
  5.0 4.4 collective-permute-start
  9.3 2.6 collective-permute-start.1
  13.0 5.9 %collective-permute-start.2 = (f32[4,1,96,128]{3,2,1,0:T(8,128)S(1)}, f32[4,1,96,128]{3,2,1,0:T(8,128)S(1)}, u32[]{:S(2)}, u32[]{:S(2)}) collective-permute-start(f32[4,1,96,128]{3,2,1,0:T(8,128)S(1)} %get-tuple-element.19), channel_id=1, source_target_pairs={{0,4},{4,8},{8,12},{1,5},{5,9},{9,13},{2,6},{6,10},{10,14},{3,7},{... | collective-permute-start | bytes 589832 | tf_op jit(solution)/shard_map/ppermute | solution.py:17
  19.0 1.9 collective-permute-start.3
  20.9 2.4 fusion.39
  23.3 2.4 collective-permute-start.5
  25.8 3.7 collective-permute-start.4
  30.3 47.0 %collective-permute-done = f32[1,64,96,128]{3,2,1,0:T(8,128)S(1)} collective-permute-done((f32[1,64,96,128]{3,2,1,0:T(8,128)S(1)}, f32[1,64,96,128]{3,2,1,0:T(8,128)S(1)}, u32[]{:S(2)}, u32[]{:S(2)}) %collective-permute-start) | collective-permute-done | bytes 3145760 | tf_op jit(solution)/shard_map/ppermute | solution.py:17
  79.2 10.3 %constant_dynamic-update-slice_fusion.1 = f32[6,64,96,128]{3,2,1,0:T(8,128)} fusion(f32[6,64,96,128]{3,2,1,0:T(8,128)} %constant_dynamic-update-slice_fusion.2, f32[4,64,96,128]{3,2,1,0:T(8,128)} %param.2), kind=kLoop, calls=%fused_computation.82 | loop fusion | bytes 25165824
  89.5 56.6 %collective-permute-done.1 = f32[1,64,96,128]{3,2,1,0:T(8,128)S(1)} collective-permute-done((f32[1,64,96,128]{3,2,1,0:T(8,128)}, f32[1,64,96,128]{3,2,1,0:T(8,128)S(1)}, u32[]{:S(2)}, u32[]{:S(2)}) %collective-permute-start.1) | collective-permute-done | bytes 3145760 | tf_op jit(solution)/shard_map/ppermute | solution.py:18
  149.7 41.2 %fusion.27 = f32[4,64,96,128]{3,2,1,0:T(8,128)} fusion(f32[4,64,96,128]{3,2,1,0:T(8,128)} %param.2, f32[4,64,1,128]{3,2,1,0:T(1,128)} %bitcast.11, f32[6,1,96,128]{3,2,1,0:T(8,128)} %pad.39, f32[6,64,96,128]{3,2,1,0:T(8,128)} %constant_dynamic-update-slice_fusion, f32[6,1,96,128]{3,2,1,0:T(8,128)S(1)} %pad.38, f32[4,64,1,128]{3,2,1,0:T(1,128)} %bitcast.9, ...), kind=kLoop, calls=%fused_computation.64 | loop fusion | flops 94371840 | bytes 63766528 | tf_op jit(solution)/shard_map/add | solution.py:46
  190.9 3.3 fusion.37
  194.2 4.4 collective-permute-start.6
  198.6 2.6 collective-permute-start.7
  202.2 7.9 %collective-permute-start.8 = (f32[4,1,96,128]{3,2,1,0:T(8,128)S(1)}, f32[4,1,96,128]{3,2,1,0:T(8,128)S(1)}, u32[]{:S(2)}, u32[]{:S(2)}) collective-permute-start(f32[4,1,96,128]{3,2,1,0:T(8,128)S(1)} %get-tuple-element.15), channel_id=1, source_target_pairs={{0,4},{4,8},{8,12},{1,5},{5,9},{9,13},{2,6},{6,10},{10,14},{3,7},{... | collective-permute-start | bytes 589832 | tf_op jit(solution)/shard_map/ppermute | solution.py:17
  210.2 1.9 collective-permute-start.9
  213.8 2.8 collective-permute-start.10
  216.7 2.6 collective-permute-start.11
  220.1 113.8 %collective-permute-done.10 = f32[4,64,1,128]{3,1,2,0:T(8,128)S(1)} collective-permute-done((f32[4,64,1,128]{3,1,2,0:T(8,128)S(1)}, f32[4,64,1,128]{3,1,2,0:T(8,128)S(1)}, u32[]{:S(2)}, u32[]{:S(2)}) %collective-permute-start.10) | collective-permute-done | bytes 131104 | tf_op jit(solution)/shard_map/ppermute | solution.py:17
  333.9 5.3 collective-permute-done.11
  340.9 45.1 %fusion.16 = f32[4,64,96,128]{3,2,1,0:T(8,128)} fusion(f32[4,64,96,128]{3,2,1,0:T(8,128)} %fusion.27, f32[4,64,1,128]{3,2,1,0:T(1,128)} %bitcast.15, f32[6,1,96,128]{3,2,1,0:T(8,128)} %pad.43, f32[6,1,96,128]{3,2,1,0:T(8,128)S(1)} %pad.42, f32[1,64,96,128]{3,2,1,0:T(8,128)} %copy-done.2, f32[1,64,96,128]{3,2,1,0:T(8,128)S(1)} %collective-permute-done.6, ...), kind=kLoop, calls=%fused_computation.35 | loop fusion | flops 119537664 | bytes 44892160 | tf_op jit(solution)/shard_map/add | solution.py:46
  386.0 3.3 fusion.34
  389.3 5.7 collective-permute-start.12
  395.0 1.9 collective-permute-start.13
  398.0 7.7 %collective-permute-start.14 = (f32[4,1,96,128]{3,2,1,0:T(8,128)S(1)}, f32[4,1,96,128]{3,2,1,0:T(8,128)S(1)}, u32[]{:S(2)}, u32[]{:S(2)}) collective-permute-start(f32[4,1,96,128]{3,2,1,0:T(8,128)S(1)} %get-tuple-element.9), channel_id=1, source_target_pairs={{0,4},{4,8},{8,12},{1,5},{5,9},{9,13},{2,6},{6,10},{10,14},{3,7},{... | collective-permute-start | bytes 589832 | tf_op jit(solution)/shard_map/ppermute | solution.py:17
  405.7 1.9 collective-permute-start.15
  409.3 1.9 collective-permute-start.16
  411.3 3.4 collective-permute-start.17
  415.4 114.5 %collective-permute-done.16 = f32[4,64,1,128]{3,1,2,0:T(8,128)S(1)} collective-permute-done((f32[4,64,1,128]{3,1,2,0:T(8,128)S(1)}, f32[4,64,1,128]{3,1,2,0:T(8,128)S(1)}, u32[]{:S(2)}, u32[]{:S(2)}) %collective-permute-start.16) | collective-permute-done | bytes 131104 | tf_op jit(solution)/shard_map/ppermute | solution.py:17
  529.9 2.8 collective-permute-done.17
  534.4 45.2 %fusion.5 = f32[4,64,96,128]{3,2,1,0:T(8,128)} fusion(f32[4,64,96,128]{3,2,1,0:T(8,128)} %fusion.16, f32[4,64,1,128]{3,2,1,0:T(1,128)} %bitcast.14, f32[6,1,96,128]{3,2,1,0:T(8,128)} %pad.47, f32[6,1,96,128]{3,2,1,0:T(8,128)S(1)} %pad.46, f32[1,64,96,128]{3,2,1,0:T(8,128)} %copy-done.1, f32[1,64,96,128]{3,2,1,0:T(8,128)S(1)} %collective-permute-done.12, ...), kind=kLoop, calls=%fused_computation.6 | loop fusion | flops 119537664 | bytes 44892160 | tf_op jit(solution)/shard_map/add | solution.py:46
  (39 shorter events, 17.7 us)
Async XLA Ops:
  5.0 72.4 %collective-permute-start = (f32[1,64,96,128]{3,2,1,0:T(8,128)S(1)}, f32[1,64,96,128]{3,2,1,0:T(8,128)S(1)}, u32[]{:S(2)}, u32[]{:S(2)}) collective-permute-start(f32[1,64,96,128]{3,2,1,0:T(8,128)S(1)} %get-tuple-element.22), channel_id=1, source_target_pairs={{0,16},{16,32},{32,48},{48,64},{64,80},{80,96},{96,112},{1,17},{17... | collective-permute-start | bytes 9437192 | tf_op jit(solution)/shard_map/ppermute | solution.py:17
  9.3 136.8 %collective-permute-start.1 = (f32[1,64,96,128]{3,2,1,0:T(8,128)}, f32[1,64,96,128]{3,2,1,0:T(8,128)S(1)}, u32[]{:S(2)}, u32[]{:S(2)}) collective-permute-start(f32[1,64,96,128]{3,2,1,0:T(8,128)} %get-tuple-element.21), channel_id=1, source_target_pairs={{16,0},{32,16},{48,32},{64,48},{80,64},{96,80},{112,96},{17,1},{33... | collective-permute-start | bytes 9437192 | tf_op jit(solution)/shard_map/ppermute | solution.py:18
  13.0 12.8 %collective-permute-start.2 = (f32[4,1,96,128]{3,2,1,0:T(8,128)S(1)}, f32[4,1,96,128]{3,2,1,0:T(8,128)S(1)}, u32[]{:S(2)}, u32[]{:S(2)}) collective-permute-start(f32[4,1,96,128]{3,2,1,0:T(8,128)S(1)} %get-tuple-element.19), channel_id=1, source_target_pairs={{0,4},{4,8},{8,12},{1,5},{5,9},{9,13},{2,6},{6,10},{10,14},{3,7},{... | collective-permute-start | bytes 589832 | tf_op jit(solution)/shard_map/ppermute | solution.py:17
  19.0 10.6 %collective-permute-start.3 = (f32[4,1,96,128]{3,2,1,0:T(8,128)S(1)}, f32[4,1,96,128]{3,2,1,0:T(8,128)S(1)}, u32[]{:S(2)}, u32[]{:S(2)}) collective-permute-start(f32[4,1,96,128]{3,2,1,0:T(8,128)S(1)} %get-tuple-element.20), channel_id=1, source_target_pairs={{4,0},{8,4},{12,8},{5,1},{9,5},{13,9},{6,2},{10,6},{14,10},{7,3},{... | collective-permute-start | bytes 589832 | tf_op jit(solution)/shard_map/ppermute | solution.py:18
  23.3 126.3 %collective-permute-start.5 = (f32[4,64,1,128]{3,1,2,0:T(8,128)}, f32[4,64,1,128]{3,1,2,0:T(8,128)}, u32[]{:S(2)}, u32[]{:S(2)}) collective-permute-start(f32[4,64,1,128]{3,1,2,0:T(8,128)} %bitcast.10), channel_id=1, source_target_pairs={{1,0},{2,1},{3,2},{5,4},{6,5},{7,6},{9,8},{10,9},{11,10},{13,12},{... | collective-permute-start | bytes 393224 | tf_op jit(solution)/shard_map/ppermute | solution.py:18
  25.8 123.9 %collective-permute-start.4 = (f32[4,64,1,128]{3,1,2,0:T(8,128)}, f32[4,64,1,128]{3,1,2,0:T(8,128)}, u32[]{:S(2)}, u32[]{:S(2)}) collective-permute-start(f32[4,64,1,128]{3,1,2,0:T(8,128)} %bitcast.8), channel_id=1, source_target_pairs={{0,1},{1,2},{2,3},{4,5},{5,6},{6,7},{8,9},{9,10},{10,11},{12,13},{... | collective-permute-start | bytes 393224 | tf_op jit(solution)/shard_map/ppermute | solution.py:17
  146.1 1.7 copy-start
  194.2 145.1 %collective-permute-start.6 = (f32[1,64,96,128]{3,2,1,0:T(8,128)S(1)}, f32[1,64,96,128]{3,2,1,0:T(8,128)S(1)}, u32[]{:S(2)}, u32[]{:S(2)}) collective-permute-start(f32[1,64,96,128]{3,2,1,0:T(8,128)S(1)} %get-tuple-element.13), channel_id=1, source_target_pairs={{0,16},{16,32},{32,48},{48,64},{64,80},{80,96},{96,112},{1,17},{17... | collective-permute-start | bytes 9437192 | tf_op jit(solution)/shard_map/ppermute | solution.py:17
  198.6 140.7 %collective-permute-start.7 = (f32[1,64,96,128]{3,2,1,0:T(8,128)S(1)}, f32[1,64,96,128]{3,2,1,0:T(8,128)S(1)}, u32[]{:S(2)}, u32[]{:S(2)}) collective-permute-start(f32[1,64,96,128]{3,2,1,0:T(8,128)S(1)} %get-tuple-element.14), channel_id=1, source_target_pairs={{16,0},{32,16},{48,32},{64,48},{80,64},{96,80},{112,96},{17,1},{33... | collective-permute-start | bytes 9437192 | tf_op jit(solution)/shard_map/ppermute | solution.py:18
  202.2 14.5 %collective-permute-start.8 = (f32[4,1,96,128]{3,2,1,0:T(8,128)S(1)}, f32[4,1,96,128]{3,2,1,0:T(8,128)S(1)}, u32[]{:S(2)}, u32[]{:S(2)}) collective-permute-start(f32[4,1,96,128]{3,2,1,0:T(8,128)S(1)} %get-tuple-element.15), channel_id=1, source_target_pairs={{0,4},{4,8},{8,12},{1,5},{5,9},{9,13},{2,6},{6,10},{10,14},{3,7},{... | collective-permute-start | bytes 589832 | tf_op jit(solution)/shard_map/ppermute | solution.py:17
  210.2 9.2 %collective-permute-start.9 = (f32[4,1,96,128]{3,2,1,0:T(8,128)S(1)}, f32[4,1,96,128]{3,2,1,0:T(8,128)S(1)}, u32[]{:S(2)}, u32[]{:S(2)}) collective-permute-start(f32[4,1,96,128]{3,2,1,0:T(8,128)S(1)} %get-tuple-element.16), channel_id=1, source_target_pairs={{4,0},{8,4},{12,8},{5,1},{9,5},{13,9},{6,2},{10,6},{14,10},{7,3},{... | collective-permute-start | bytes 589832 | tf_op jit(solution)/shard_map/ppermute | solution.py:18
  213.8 120.1 %collective-permute-start.10 = (f32[4,64,1,128]{3,1,2,0:T(8,128)S(1)}, f32[4,64,1,128]{3,1,2,0:T(8,128)S(1)}, u32[]{:S(2)}, u32[]{:S(2)}) collective-permute-start(f32[4,64,1,128]{3,1,2,0:T(8,128)S(1)} %bitcast.19), channel_id=1, source_target_pairs={{0,1},{1,2},{2,3},{4,5},{5,6},{6,7},{8,9},{9,10},{10,11},{12,13},{... | collective-permute-start | bytes 393224 | tf_op jit(solution)/shard_map/ppermute | solution.py:17
  216.7 122.6 %collective-permute-start.11 = (f32[4,64,1,128]{3,1,2,0:T(8,128)S(1)}, f32[4,64,1,128]{3,1,2,0:T(8,128)S(1)}, u32[]{:S(2)}, u32[]{:S(2)}) collective-permute-start(f32[4,64,1,128]{3,1,2,0:T(8,128)S(1)} %bitcast.17), channel_id=1, source_target_pairs={{1,0},{2,1},{3,2},{5,4},{6,5},{7,6},{9,8},{10,9},{11,10},{13,12},{... | collective-permute-start | bytes 393224 | tf_op jit(solution)/shard_map/ppermute | solution.py:18
  333.9 7.0 %copy-start.4 = (f32[4,64,1,128]{3,1,2,0:T(8,128)}, f32[4,64,1,128]{3,1,2,0:T(8,128)S(1)}, u32[]{:S(2)}) copy-start(f32[4,64,1,128]{3,1,2,0:T(8,128)S(1)} %collective-permute-done.10) | copy-start | bytes 393220
  339.3 1.7 copy-start.6
  339.3 1.7 copy-start.2
  389.3 143.4 %collective-permute-start.12 = (f32[1,64,96,128]{3,2,1,0:T(8,128)S(1)}, f32[1,64,96,128]{3,2,1,0:T(8,128)S(1)}, u32[]{:S(2)}, u32[]{:S(2)}) collective-permute-start(f32[1,64,96,128]{3,2,1,0:T(8,128)S(1)} %get-tuple-element.7), channel_id=1, source_target_pairs={{0,16},{16,32},{32,48},{48,64},{64,80},{80,96},{96,112},{1,17},{17... | collective-permute-start | bytes 9437192 | tf_op jit(solution)/shard_map/ppermute | solution.py:17
  395.0 137.8 %collective-permute-start.13 = (f32[1,64,96,128]{3,2,1,0:T(8,128)S(1)}, f32[1,64,96,128]{3,2,1,0:T(8,128)S(1)}, u32[]{:S(2)}, u32[]{:S(2)}) collective-permute-start(f32[1,64,96,128]{3,2,1,0:T(8,128)S(1)} %get-tuple-element.8), channel_id=1, source_target_pairs={{16,0},{32,16},{48,32},{64,48},{80,64},{96,80},{112,96},{17,1},{33... | collective-permute-start | bytes 9437192 | tf_op jit(solution)/shard_map/ppermute | solution.py:18
  398.0 13.3 %collective-permute-start.14 = (f32[4,1,96,128]{3,2,1,0:T(8,128)S(1)}, f32[4,1,96,128]{3,2,1,0:T(8,128)S(1)}, u32[]{:S(2)}, u32[]{:S(2)}) collective-permute-start(f32[4,1,96,128]{3,2,1,0:T(8,128)S(1)} %get-tuple-element.9), channel_id=1, source_target_pairs={{0,4},{4,8},{8,12},{1,5},{5,9},{9,13},{2,6},{6,10},{10,14},{3,7},{... | collective-permute-start | bytes 589832 | tf_op jit(solution)/shard_map/ppermute | solution.py:17
  405.7 9.0 %collective-permute-start.15 = (f32[4,1,96,128]{3,2,1,0:T(8,128)S(1)}, f32[4,1,96,128]{3,2,1,0:T(8,128)S(1)}, u32[]{:S(2)}, u32[]{:S(2)}) collective-permute-start(f32[4,1,96,128]{3,2,1,0:T(8,128)S(1)} %get-tuple-element.10), channel_id=1, source_target_pairs={{4,0},{8,4},{12,8},{5,1},{9,5},{13,9},{6,2},{10,6},{14,10},{7,3},{... | collective-permute-start | bytes 589832 | tf_op jit(solution)/shard_map/ppermute | solution.py:18
  409.3 120.6 %collective-permute-start.16 = (f32[4,64,1,128]{3,1,2,0:T(8,128)S(1)}, f32[4,64,1,128]{3,1,2,0:T(8,128)S(1)}, u32[]{:S(2)}, u32[]{:S(2)}) collective-permute-start(f32[4,64,1,128]{3,1,2,0:T(8,128)S(1)} %bitcast.18), channel_id=1, source_target_pairs={{0,1},{1,2},{2,3},{4,5},{5,6},{6,7},{8,9},{9,10},{10,11},{12,13},{... | collective-permute-start | bytes 393224 | tf_op jit(solution)/shard_map/ppermute | solution.py:17
  411.3 121.4 %collective-permute-start.17 = (f32[4,64,1,128]{3,1,2,0:T(8,128)S(1)}, f32[4,64,1,128]{3,1,2,0:T(8,128)S(1)}, u32[]{:S(2)}, u32[]{:S(2)}) collective-permute-start(f32[4,64,1,128]{3,1,2,0:T(8,128)S(1)} %bitcast.16), channel_id=1, source_target_pairs={{1,0},{2,1},{3,2},{5,4},{6,5},{7,6},{9,8},{10,9},{11,10},{13,12},{... | collective-permute-start | bytes 393224 | tf_op jit(solution)/shard_map/ppermute | solution.py:18
  529.9 4.5 copy-start.3
  532.7 1.7 copy-start.5
  532.7 1.7 copy-start.1
where the time goes:
time: 585 us; the launch traced here: 580 us
  waiting for transfers between devices  340 us (58%)
  other arithmetic  131 us (22%)
  starting transfers between devices  65.8 us (11%)
  local copies, waits for them, and re-layouts  42 us (7%)
    ppermute x9, waiting for transfers between devices, extended(): lax.ppermute(last, axis, up)  275 us
    add x3, other arithmetic, advance_population(): return middle + 0.1 * spread + 0.2 * middle * (1.0 - middle * inverse_limit)  131 us
    ppermute x9, waiting for transfers between devices, extended(): lax.ppermute(leading, axis, [(b, a) for a, b in up])  64.7 us
    ppermute x9, starting transfers between devices, extended(): lax.ppermute(last, axis, up)  44.5 us
    ppermute x9, starting transfers between devices, extended(): lax.ppermute(leading, axis, [(b, a) for a, b in up])  21.3 us
    unnamed x16, local copies, waits for them, and re-layouts  17.2 us
    slice x8, local copies, waits for them, and re-layouts, extended(): last = lax.slice_in_dim(x, length - width, length, axis=dim)  15.7 us
  transfers between devices with their start and end apart: 18, of which 6 were waited for; matrix products, arithmetic and copies ran while one was open for 4% of the time, Pallas kernels for 0%

commit v1 on v0

v1 whole, which is shorter than its diff:
```python
import functools

import jax
import jax.numpy as jnp
from jax import lax
from jax.experimental import pallas as pl
from jax.experimental.pallas import tpu as pltpu
from jax.sharding import PartitionSpec as P

STEPS = 3
ROWS = 8
MESH = pl.DeviceIdType.MESH


def kernel(sizes, u_ref, inv_ref, out_ref, buf, inv, halo, pz_in, pz_out,
           load_sem, store_sem, py_send, py_recv, px_send, px_recv, pz_send, pz_recv):
    planes, rows, cols, _ = u_ref.shape
    chunks = rows // ROWS
    me = {axis: lax.axis_index(axis) for axis in sizes}

    def there(axis, side):
        return me[axis] > 0 if side == 0 else me[axis] < sizes[axis] - 1

    def peer(axis, side):
        return {axis: me[axis] + (1 if side else -1)}

    loads = [
        pltpu.make_async_copy(u_ref, buf.at[0, :, pl.ds(1, rows)], load_sem.at[0]),
        pltpu.make_async_copy(inv_ref, inv, load_sem.at[1]),
    ]
    for load in loads:
        load.start()

    barrier = pltpu.get_barrier_semaphore()
    for axis in sizes:
        for side in (0, 1):
            @pl.when(there(axis, side))
            def _():
                pl.semaphore_signal(barrier, inc=1, device_id=peer(axis, side), device_id_type=MESH)
    peers = sum(there(axis, side).astype(jnp.int32) for axis in sizes for side in (0, 1))
    pl.semaphore_wait(barrier, peers)

    def py_copy(step, side, k, with_side=None):
        face = 0 if side == 0 else planes - 1
        at = pl.multiple_of(k * ROWS, ROWS)
        if step == 0:
            src = u_ref.at[face, pl.ds(at, ROWS)]
        else:
            src = buf.at[step % 2, face, pl.ds(at + 1, ROWS)]
        return pltpu.make_async_remote_copy(
            src_ref=src, dst_ref=halo.at[step, 1 - side, pl.ds(at, ROWS)],
            send_sem=py_send.at[step, side, k], recv_sem=py_recv.at[step, 1 - side, k],
            device_id=peer("py", side if with_side is None else with_side), device_id_type=MESH)

    def px_copy(step, side, with_side=None):
        edge = 0 if side == 0 else rows - 1
        src = u_ref.at[:, edge] if step == 0 else buf.at[step % 2, :, edge + 1]
        return pltpu.make_async_remote_copy(
            src_ref=src, dst_ref=buf.at[step % 2, :, rows + 1 if side == 0 else 0],
            send_sem=px_send.at[step, side], recv_sem=px_recv.at[step, 1 - side],
            device_id=peer("px", side if with_side is None else with_side), device_id_type=MESH)

    def pz_copy(step, side, with_side=None):
        return pltpu.make_async_remote_copy(
            src_ref=pz_out.at[step, side], dst_ref=pz_in.at[step, 1 - side],
            send_sem=pz_send.at[step, side], recv_sem=pz_recv.at[step, 1 - side],
            device_id=peer("pz", side if with_side is None else with_side), device_id_type=MESH)

    def store(k):
        at = pl.multiple_of(k * ROWS, ROWS)
        return pltpu.make_async_copy(
            buf.at[STEPS % 2, :, pl.ds(at + 1, ROWS)], out_ref.at[:, pl.ds(at, ROWS)], store_sem.at[k])

    for side in (0, 1):
        @pl.when(there("px", side))
        def _():
            px_copy(0, side).start()

    def first_sends(k, carry):
        for side in (0, 1):
            @pl.when(there("py", side))
            def _():
                py_copy(0, side, k).start()
        return carry
    lax.fori_loop(0, chunks, first_sends, 0)

    for side in (0, 1):
        @pl.when(jnp.logical_not(there("py", side)))
        def _():
            def clear(r, carry):
                for step in range(STEPS):
                    halo[step, side, r] = jnp.zeros(halo.shape[3:], halo.dtype)
                return carry
            lax.fori_loop(0, rows, clear, 0)

        @pl.when(jnp.logical_not(there("px", side)))
        def _():
            for slot in (0, 1):
                for p in range(planes):
                    buf[slot, p, 0 if side == 0 else rows + 1] = jnp.zeros(buf.shape[3:], buf.dtype)

        @pl.when(jnp.logical_not(there("pz", side)))
        def _():
            for step in range(STEPS):
                for p in range(planes):
                    pz_in[step, side, p] = jnp.zeros(pz_in.shape[3:], pz_in.dtype)

    loads[0].wait()

    def pack(r, carry):
        for p in range(planes):
            pz_out[0, 0, p, pl.ds(r, 1)] = buf[0, p, r + 1, 0:1]
            pz_out[0, 1, p, pl.ds(r, 1)] = buf[0, p, r + 1, cols - 1:cols]
        return carry
    lax.fori_loop(0, rows, pack, 0)
    for side in (0, 1):
        @pl.when(there("pz", side))
        def _():
            pz_copy(0, side).start()
    loads[1].wait()

    for step in range(STEPS):
        now, later = step % 2, (step + 1) % 2
        for side in (0, 1):
            @pl.when(there("px", side))
            def _():
                px_copy(step, side).wait_send()
                px_copy(step, 1 - side, side).wait_recv()

            @pl.when(there("pz", side))
            def _():
                pz_copy(step, side).wait_send()
                pz_copy(step, 1 - side, side).wait_recv()

        def chunk(k, carry):
            for side in (0, 1):
                @pl.when(there("py", side))
                def _():
                    py_copy(step, 1 - side, k, side).wait_recv()
                    if step >= 1:
                        py_copy(step - 1, side, k).wait_send()

            def row(i, inner):
                r = k * ROWS + i
                for p in range(planes):
                    mid = buf[now, p, r + 1]
                    lower = halo[step, 0, r] if p == 0 else buf[now, p - 1, r + 1]
                    upper = halo[step, 1, r] if p == planes - 1 else buf[now, p + 1, r + 1]
                    left = jnp.concatenate([pz_in[step, 0, p, pl.ds(r, 1)], mid[:-1]], axis=0)
                    right = jnp.concatenate([mid[1:], pz_in[step, 1, p, pl.ds(r, 1)]], axis=0)
                    spread = lower + upper + buf[now, p, r] + buf[now, p, r + 2] + left + right - 6.0 * mid
                    new = mid + 0.1 * spread + 0.2 * mid * (1.0 - mid * inv[p, r])
                    buf[later, p, r + 1] = new
                    if step < STEPS - 1:
                        pz_out[step + 1, 0, p, pl.ds(r, 1)] = new[0:1]
                        pz_out[step + 1, 1, p, pl.ds(r, 1)] = new[cols - 1:cols]
                return inner
            lax.fori_loop(0, ROWS, row, 0)

            if step < STEPS - 1:
                for side in (0, 1):
                    @pl.when(there("py", side))
                    def _():
                        py_copy(step + 1, side, k).start()
            else:
                store(k).start()
            return carry
        lax.fori_loop(0, chunks, chunk, 0)

        if step < STEPS - 1:
            for side in (0, 1):
                @pl.when(there("px", side))
                def _():
                    px_copy(step + 1, side).start()

                @pl.when(there("pz", side))
                def _():
                    pz_copy(step + 1, side).start()

    def finish(k, carry):
        for side in (0, 1):
            @pl.when(there("py", side))
            def _():
                py_copy(STEPS - 1, side, k).wait_send()
        store(k).wait()
        return carry
    lax.fori_loop(0, chunks, finish, 0)


def local(sizes, u, inv):
    planes, rows, cols, levels = u.shape
    chunks = rows // ROWS
    dma = pltpu.SemaphoreType.DMA
    return pl.pallas_call(
        functools.partial(kernel, sizes),
        out_shape=jax.ShapeDtypeStruct(u.shape, u.dtype),
        in_specs=[pl.BlockSpec(memory_space=pl.ANY)] * 2,
        out_specs=pl.BlockSpec(memory_space=pl.ANY),
        scratch_shapes=[
            pltpu.VMEM((2, planes, rows + 2, cols, levels), u.dtype),
            pltpu.VMEM(u.shape, u.dtype),
            pltpu.VMEM((STEPS, 2, rows, cols, levels), u.dtype),
            pltpu.VMEM((STEPS, 2, planes, rows, levels), u.dtype),
            pltpu.VMEM((STEPS, 2, planes, rows, levels), u.dtype),
            dma((2,)),
            dma((chunks,)),
            dma((STEPS, 2, chunks)),
            dma((STEPS, 2, chunks)),
            dma((STEPS, 2)),
            dma((STEPS, 2)),
            dma((STEPS, 2)),
            dma((STEPS, 2)),
        ],
        compiler_params=pltpu.CompilerParams(
            collective_id=0, has_side_effects=True, vmem_limit_bytes=67043328),
    )(u, inv)


def solution(mesh):
    spec = P("py", "px", "pz", None)
    sizes = {axis: mesh.shape[axis] for axis in ("py", "px", "pz")}
    return jax.shard_map(functools.partial(local, sizes), mesh=mesh, in_specs=(spec, spec),
                         out_specs=spec, check_vma=False)
```

time: 585 us -> 452 us (0.77)
  Pallas kernels: 0 us -> 438 us
  waiting for transfers between devices: 340 us -> 0 us
  other arithmetic: 131 us -> 0 us
  starting transfers between devices: 65.8 us -> 0 us
  local copies, waits for them, and re-layouts: 42 us -> 10.6 us
    pallas_call x0 -> x1, Pallas kernels: none -> 438 us  [local(): pl.pallas_call(functools.partial(kernel, sizes), out_shape=jax.ShapeDtype...]
    ppermute x18 -> x0, waiting for transfers between devices: 340 us -> none  [the longest x9 275 us: extended(): lax.ppermute(last, axis, up)]
    add x3 -> x0, other arithmetic: 131 us -> none  [advance_population(): return middle + 0.1 * spread + 0.2 * middle * (1.0 - middle * inverse_limit)]
    ppermute x18 -> x0, starting transfers between devices: 65.8 us -> none  [the longest x9 44.5 us: extended(): lax.ppermute(last, axis, up)]
    slice x9 -> x0, local copies, waits for them, and re-layouts: 20.6 us -> none  [the longest x8 15.7 us: extended(): last = lax.slice_in_dim(x, length - width, length, axis=dim)]
    unnamed x16 -> x1, local copies, waits for them, and re-layouts: 17.2 us -> 10.6 us
  transfers between devices with their start and end apart: 18 -> 0, of which waited for: 6 -> 0; matrix products, arithmetic and copies ran while one was open for 4% -> 0% of each run, Pallas kernels for 0% -> 0%
where the time goes in v1:
time: 452 us; the launch traced here: 448 us
  Pallas kernels  438 us (97%)
  local copies, waits for them, and re-layouts  10.6 us (2%)
    pallas_call x1, Pallas kernels, local(): pl.pallas_call(functools.partial(kernel, sizes), out_shape=jax.ShapeDtype...  438 us
    unnamed x1, local copies, waits for them, and re-layouts  10.6 us

profile of v1, /device:TPU:7, one launch (start us, length us, event | category | flops | bytes accessed | tf_op | source)
XLA Modules:
  0.0 448.3 jit_solution(4869846982519402113)
XLA Ops:
  0.0 437.6 %shard_map.28 = f32[4,64,96,128]{3,2,1,0:T(8,128)} custom-call(f32[4,64,96,128]{3,2,1,0:T(8,128)} %u_ref.1, f32[4,64,96,128]{3,2,1,0:T(8,128)} %inv_ref.1), custom_call_target="tpu_custom_call" | custom-call | tf_op jit(solution)/shard_map/pallas_call | solution.py:194
  437.7 10.6 %copy.4 = f32[4,64,96,128]{3,2,1,0:T(8,128)} copy(f32[4,64,96,128]{3,2,1,0:T(8,128)} %shard_map.28) | data formatting | bytes 25165824

commit v2 on v1

--- a/solution.py
+++ b/solution.py
@@ -12,11 +12,21 @@
 MESH = pl.DeviceIdType.MESH
 
 
-def kernel(sizes, u_ref, inv_ref, out_ref, buf, inv, halo, pz_in, pz_out,
-           load_sem, store_sem, py_send, py_recv, px_send, px_recv, pz_send, pz_recv):
+def share(n, k):
+    return k % 4 < n
+
+
+def kernel(sizes, u_ref, inv_ref, out_ref, transit, buf, inv, halo, pz_in, pz_out,
+           load_sem, store_sem, py_send, py_recv, px_send, px_recv, pz_send, pz_recv,
+           via_send, via_recv):
     planes, rows, cols, _ = u_ref.shape
     chunks = rows // ROWS
+    ahead = chunks // 2
     me = {axis: lax.axis_index(axis) for axis in sizes}
+    last = sizes["py"] - 1
+    parity = [me["py"] % 2 == 0, me["py"] % 2 == 1]
+    mine = ((last + 1 - me["py"]) // 2, (me["py"] + 1) // 2)
+    others = ((last - 1 - me["py"]) // 2, (me["py"] - 1) // 2)
 
     def there(axis, side):
         return me[axis] > 0 if side == 0 else me[axis] < sizes[axis] - 1
@@ -32,25 +42,48 @@
         load.start()
 
     barrier = pltpu.get_barrier_semaphore()
+    peers = jnp.int32(0)
     for axis in sizes:
         for side in (0, 1):
+            peers += there(axis, side).astype(jnp.int32)
+
             @pl.when(there(axis, side))
             def _():
                 pl.semaphore_signal(barrier, inc=1, device_id=peer(axis, side), device_id_type=MESH)
-    peers = sum(there(axis, side).astype(jnp.int32) for axis in sizes for side in (0, 1))
+    for far, exists in ((me["py"] - 2, me["py"] > 1), (me["py"] + 2, me["py"] < last - 1)):
+        peers += exists.astype(jnp.int32)
+
+        @pl.when(exists)
+        def _():
+            pl.semaphore_signal(barrier, inc=1, device_id={"py": far}, device_id_type=MESH)
     pl.semaphore_wait(barrier, peers)
 
-    def py_copy(step, side, k, with_side=None):
+    def source(step, side, k):
         face = 0 if side == 0 else planes - 1
         at = pl.multiple_of(k * ROWS, ROWS)
         if step == 0:
-            src = u_ref.at[face, pl.ds(at, ROWS)]
-        else:
-            src = buf.at[step % 2, face, pl.ds(at + 1, ROWS)]
-        return pltpu.make_async_remote_copy(
-            src_ref=src, dst_ref=halo.at[step, 1 - side, pl.ds(at, ROWS)],
+            return u_ref.at[face, pl.ds(at, ROWS)]
+        return buf.at[step % 2, face, pl.ds(at + 1, ROWS)]
+
+    def py_copy(step, side, k, device=None):
+        at = pl.multiple_of(k * ROWS, ROWS)
+        return pltpu.make_async_remote_copy(
+            src_ref=source(step, side, k), dst_ref=halo.at[step, 1 - side, pl.ds(at, ROWS)],
             send_sem=py_send.at[step, side, k], recv_sem=py_recv.at[step, 1 - side, k],
-            device_id=peer("py", side if with_side is None else with_side), device_id_type=MESH)
+            device_id=peer("py", side) if device is None else device, device_id_type=MESH)
+
+    def via_copy(step, q, k):
+        return pltpu.make_async_remote_copy(
+            src_ref=source(step, q, k), dst_ref=transit.at[step, k],
+            send_sem=py_send.at[step, q, k], recv_sem=via_recv.at[step, k],
+            device_id={"py": me["py"] + (2 if q else -2)}, device_id_type=MESH)
+
+    def on_copy(step, q, k):
+        at = pl.multiple_of(k * ROWS, ROWS)
+        return pltpu.make_async_remote_copy(
+            src_ref=transit.at[step, k], dst_ref=halo.at[step, 1 - q, pl.ds(at, ROWS)],
+            send_sem=via_send.at[step, k], recv_sem=py_recv.at[step, 1 - q, k],
+            device_id=peer("py", 1 - q), device_id_type=MESH)
 
     def px_copy(step, side, with_side=None):
         edge = 0 if side == 0 else rows - 1
@@ -71,28 +104,54 @@
         return pltpu.make_async_copy(
             buf.at[STEPS % 2, :, pl.ds(at + 1, ROWS)], out_ref.at[:, pl.ds(at, ROWS)], store_sem.at[k])
 
+    def goes_via(q, k):
+        return jnp.logical_and(jnp.logical_and(parity[q], there("py", q)), share(mine[q], k))
+
+    def held(q, k):
+        return jnp.logical_and(parity[q], share(others[q], k))
+
+    def send_early(step, k):
+        for q in (0, 1):
+            @pl.when(goes_via(q, k))
+            def _():
+                via_copy(step, q, k).start()
+
+    def send(step, k):
+        for q in (0, 1):
+            @pl.when(jnp.logical_and(there("py", q), jnp.logical_not(goes_via(q, k))))
+            def _():
+                py_copy(step, q, k).start()
+
+            @pl.when(held(q, k))
+            def _():
+                via_copy(step, q, k).wait_recv()
+                on_copy(step, q, k).start()
+
+    def sent(step, k):
+        for q in (0, 1):
+            @pl.when(there("py", q))
+            def _():
+                py_copy(step, q, k).wait_send()
+
+            @pl.when(held(q, k))
+            def _():
+                on_copy(step, q, k).wait_send()
+
     for side in (0, 1):
         @pl.when(there("px", side))
         def _():
             px_copy(0, side).start()
 
-    def first_sends(k, carry):
-        for side in (0, 1):
-            @pl.when(there("py", side))
-            def _():
-                py_copy(0, side, k).start()
-        return carry
-    lax.fori_loop(0, chunks, first_sends, 0)
+    def loop(count, body, start=0):
+        def step(k, carry):
+            body(k)
+            return carry
+        lax.fori_loop(start, count, step, 0)
+
+    loop(chunks, lambda k: send_early(0, k))
+    loop(ahead, lambda k: send(0, k))
 
     for side in (0, 1):
-        @pl.when(jnp.logical_not(there("py", side)))
-        def _():
-            def clear(r, carry):
-                for step in range(STEPS):
-                    halo[step, side, r] = jnp.zeros(halo.shape[3:], halo.dtype)
-                return carry
-            lax.fori_loop(0, rows, clear, 0)
-
         @pl.when(jnp.logical_not(there("px", side)))
         def _():
             for slot in (0, 1):
@@ -107,18 +166,18 @@
 
     loads[0].wait()
 
-    def pack(r, carry):
+    def pack(r):
         for p in range(planes):
             pz_out[0, 0, p, pl.ds(r, 1)] = buf[0, p, r + 1, 0:1]
             pz_out[0, 1, p, pl.ds(r, 1)] = buf[0, p, r + 1, cols - 1:cols]
-        return carry
-    lax.fori_loop(0, rows, pack, 0)
+    loop(rows, pack)
     for side in (0, 1):
         @pl.when(there("pz", side))
         def _():
             pz_copy(0, side).start()
     loads[1].wait()
 
+    inside = [there("py", side) for side in (0, 1)]
     for step in range(STEPS):
         now, later = step % 2, (step + 1) % 2
         for side in (0, 1):
@@ -132,20 +191,22 @@
                 pz_copy(step, side).wait_send()
                 pz_copy(step, 1 - side, side).wait_recv()
 
-        def chunk(k, carry):
+        def chunk(k, half):
+            if half == 0:
+                send(step, k + ahead)
             for side in (0, 1):
                 @pl.when(there("py", side))
                 def _():
-                    py_copy(step, 1 - side, k, side).wait_recv()
-                    if step >= 1:
-                        py_copy(step - 1, side, k).wait_send()
-
-            def row(i, inner):
+                    py_copy(step, 1 - side, k, peer("py", side)).wait_recv()
+            if step >= 1:
+                sent(step - 1, k)
+
+            def row(i):
                 r = k * ROWS + i
                 for p in range(planes):
                     mid = buf[now, p, r + 1]
-                    lower = halo[step, 0, r] if p == 0 else buf[now, p - 1, r + 1]
-                    upper = halo[step, 1, r] if p == planes - 1 else buf[now, p + 1, r + 1]
+                    lower = jnp.where(inside[0], halo[step, 0, r], 0.0) if p == 0 else buf[now, p - 1, r + 1]
+                    upper = jnp.where(inside[1], halo[step, 1, r], 0.0) if p == planes - 1 else buf[now, p + 1, r + 1]
                     left = jnp.concatenate([pz_in[step, 0, p, pl.ds(r, 1)], mid[:-1]], axis=0)
                     right = jnp.concatenate([mid[1:], pz_in[step, 1, p, pl.ds(r, 1)]], axis=0)
                     spread = lower + upper + buf[now, p, r] + buf[now, p, r + 2] + left + right - 6.0 * mid
@@ -154,18 +215,17 @@
                     if step < STEPS - 1:
                         pz_out[step + 1, 0, p, pl.ds(r, 1)] = new[0:1]
                         pz_out[step + 1, 1, p, pl.ds(r, 1)] = new[cols - 1:cols]
-                return inner
-            lax.fori_loop(0, ROWS, row, 0)
+            loop(ROWS, row)
 
             if step < STEPS - 1:
-                for side in (0, 1):
-                    @pl.when(there("py", side))
-                    def _():
-                        py_copy(step + 1, side, k).start()
+                send_early(step + 1, k)
+                if half == 1:
+                    send(step + 1, k - ahead)
             else:
                 store(k).start()
-            return carry
-        lax.fori_loop(0, chunks, chunk, 0)
+
+        loop(ahead, lambda k: chunk(k, 0))
+        loop(chunks, lambda k: chunk(k, 1), ahead)
 
         if step < STEPS - 1:
             for side in (0, 1):
@@ -177,14 +237,10 @@
                 def _():
                     pz_copy(step + 1, side).start()
 
-    def finish(k, carry):
-        for side in (0, 1):
-            @pl.when(there("py", side))
-            def _():
-                py_copy(STEPS - 1, side, k).wait_send()
+    def finish(k):
+        sent(STEPS - 1, k)
         store(k).wait()
-        return carry
-    lax.fori_loop(0, chunks, finish, 0)
+    loop(chunks, finish)
 
 
 def local(sizes, u, inv):
@@ -193,9 +249,10 @@
     dma = pltpu.SemaphoreType.DMA
     return pl.pallas_call(
         functools.partial(kernel, sizes),
-        out_shape=jax.ShapeDtypeStruct(u.shape, u.dtype),
+        out_shape=(jax.ShapeDtypeStruct(u.shape, u.dtype),
+                   jax.ShapeDtypeStruct((STEPS, chunks, ROWS, cols, levels), u.dtype)),
         in_specs=[pl.BlockSpec(memory_space=pl.ANY)] * 2,
-        out_specs=pl.BlockSpec(memory_space=pl.ANY),
+        out_specs=(pl.BlockSpec(memory_space=pl.ANY),) * 2,
         scratch_shapes=[
             pltpu.VMEM((2, planes, rows + 2, cols, levels), u.dtype),
             pltpu.VMEM(u.shape, u.dtype),
@@ -210,10 +267,12 @@
             dma((STEPS, 2)),
             dma((STEPS, 2)),
             dma((STEPS, 2)),
+            dma((STEPS, chunks)),
+            dma((STEPS, chunks)),
         ],
         compiler_params=pltpu.CompilerParams(
             collective_id=0, has_side_effects=True, vmem_limit_bytes=67043328),
-    )(u, inv)
+    )(u, inv)[0]
 
 
 def solution(mesh):

time: 452 us -> 406 us (0.90)
  Pallas kernels: 438 us -> 392 us
    pallas_call x1, Pallas kernels: 438 us -> 392 us  [local(): pl.pallas_call(functools.partial(kernel, sizes), out_shape=(jax.ShapeDtyp...]
where the time goes in v2:
time: 406 us; the launch traced here: 403 us
  Pallas kernels  392 us (97%)
  local copies, waits for them, and re-layouts  10.6 us (3%)
    pallas_call x1, Pallas kernels, local(): pl.pallas_call(functools.partial(kernel, sizes), out_shape=(jax.ShapeDtyp...  392 us
    unnamed x1, local copies, waits for them, and re-layouts  10.6 us

profile of v2, /device:TPU:7, one launch (start us, length us, event | category | flops | bytes accessed | tf_op | source)
XLA Modules:
  0.0 402.7 jit_solution(14743598619081287094)
XLA Ops:
  0.0 392.1 %shard_map.28 = (f32[4,64,96,128]{3,2,1,0:T(8,128)}, f32[3,8,8,96,128]{4,3,2,1,0:T(8,128)}) custom-call(f32[4,64,96,128]{3,2,1,0:T(8,128)} %u_ref.1, f32[4,64,96,128]{3,2,1,0:T(8,128)} %inv_ref.1), custom_call_target="tpu_custom_call" | custom-call | tf_op jit(solution)/shard_map/pallas_call | solution.py:250
  392.1 10.6 %copy.4 = f32[4,64,96,128]{3,2,1,0:T(8,128)} copy(f32[4,64,96,128]{3,2,1,0:T(8,128)} %get-tuple-element.6) | data formatting | bytes 25165824

commit v3 on v2

v3 whole, which is shorter than its diff:
```python
import functools

import jax
import jax.numpy as jnp
from jax import lax
from jax.experimental import pallas as pl
from jax.experimental.pallas import tpu as pltpu
from jax.sharding import PartitionSpec as P

STEPS = 3
ROWS = 4
AHEAD = 8
EARLY = 2
MESH = pl.DeviceIdType.MESH


def share(n, k):
    return k % 4 < n


def half(k):
    return k % 2 == 1


def kernel(sizes, u_ref, inv_ref, out_ref, transit, buf0, inv, halo, pz_in, pz_out,
           load_sem, py_send, py_recv, px_send, px_recv, pz_send, pz_recv,
           via_send, via_recv, pz_transit, pz_via_send, pz_via_recv):
    planes, rows, cols, _ = u_ref.shape
    chunks = rows // ROWS
    bufs = (buf0, out_ref)
    me = {axis: lax.axis_index(axis) for axis in sizes}
    last = sizes["py"] - 1
    parity = [me["py"] % 2 == 0, me["py"] % 2 == 1]
    mine = ((last + 1 - me["py"]) // 2, (me["py"] + 1) // 2)
    others = ((last - 1 - me["py"]) // 2, (me["py"] - 1) // 2)

    def there(axis, side):
        return me[axis] > 0 if side == 0 else me[axis] < sizes[axis] - 1

    def peer(axis, side):
        return {axis: me[axis] + (1 if side else -1)}

    def loop(count, body, start=0):
        def step(k, carry):
            body(k)
            return carry
        lax.fori_loop(start, count, step, 0)

    loads = [
        pltpu.make_async_copy(u_ref, buf0.at[:, pl.ds(1, rows)], load_sem.at[0]),
        pltpu.make_async_copy(inv_ref, inv, load_sem.at[1]),
    ]
    for load in loads:
        load.start()

    barrier = pltpu.get_barrier_semaphore()
    peers = jnp.int32(0)
    for axis in sizes:
        for side in (0, 1):
            peers += there(axis, side).astype(jnp.int32)

            @pl.when(there(axis, side))
            def _():
                pl.semaphore_signal(barrier, inc=1, device_id=peer(axis, side), device_id_type=MESH)
    for axis in ("py", "pz"):
        for far, exists in ((me[axis] - 2, me[axis] > 1), (me[axis] + 2, me[axis] < sizes[axis] - 2)):
            peers += exists.astype(jnp.int32)

            @pl.when(exists)
            def _():
                pl.semaphore_signal(barrier, inc=1, device_id={axis: far}, device_id_type=MESH)
    pl.semaphore_wait(barrier, peers)

    def source(step, side, k):
        face = 0 if side == 0 else planes - 1
        at = pl.multiple_of(k * ROWS, ROWS)
        if step == 0:
            return u_ref.at[face, pl.ds(at, ROWS)]
        return bufs[step % 2].at[face, pl.ds(at + 1, ROWS)]

    def py_copy(step, side, k, device=None):
        at = pl.multiple_of(k * ROWS, ROWS)
        return pltpu.make_async_remote_copy(
            src_ref=source(step, side, k), dst_ref=halo.at[step, 1 - side, pl.ds(at, ROWS)],
            send_sem=py_send.at[step, side, k], recv_sem=py_recv.at[step, 1 - side, k],
            device_id=peer("py", side) if device is None else device, device_id_type=MESH)

    def via_copy(step, q, k):
        return pltpu.make_async_remote_copy(
            src_ref=source(step, q, k), dst_ref=transit.at[step, k],
            send_sem=py_send.at[step, q, k], recv_sem=via_recv.at[step, k],
            device_id={"py": me["py"] + (2 if q else -2)}, device_id_type=MESH)

    def on_copy(step, q, k):
        at = pl.multiple_of(k * ROWS, ROWS)
        return pltpu.make_async_remote_copy(
            src_ref=transit.at[step, k], dst_ref=halo.at[step, 1 - q, pl.ds(at, ROWS)],
            send_sem=via_send.at[step, k], recv_sem=py_recv.at[step, 1 - q, k],
            device_id=peer("py", 1 - q), device_id_type=MESH)

    def px_copy(step, side, device=None):
        edge = 0 if side == 0 else rows - 1
        src = u_ref.at[:, edge] if step == 0 else bufs[step % 2].at[:, edge + 1]
        return pltpu.make_async_remote_copy(
            src_ref=src, dst_ref=bufs[step % 2].at[:, rows + 1 if side == 0 else 0],
            send_sem=px_send.at[step, side], recv_sem=px_recv.at[step, 1 - side],
            device_id=peer("px", side) if device is None else device, device_id_type=MESH)

    def pz_copy(step, side, k, device=None):
        return pltpu.make_async_remote_copy(
            src_ref=pz_out.at[step, side, k], dst_ref=pz_in.at[step, 1 - side, k],
            send_sem=pz_send.at[step, side, k], recv_sem=pz_recv.at[step, 1 - side, k],
            device_id=peer("pz", side) if device is None else device, device_id_type=MESH)

    def pz_via_copy(step, q, k):
        return pltpu.make_async_remote_copy(
            src_ref=pz_out.at[step, q, k], dst_ref=pz_transit.at[step, k],
            send_sem=pz_send.at[step, q, k], recv_sem=pz_via_recv.at[step, k],
            device_id={"pz": me["pz"] + (2 if q else -2)}, device_id_type=MESH)

    def pz_on_copy(step, q, k):
        return pltpu.make_async_remote_copy(
            src_ref=pz_transit.at[step, k], dst_ref=pz_in.at[step, 1 - q, k],
            send_sem=pz_via_send.at[step, k], recv_sem=pz_recv.at[step, 1 - q, k],
            device_id=peer("pz", 1 - q), device_id_type=MESH)

    pz_sender = (me["pz"] == 2, me["pz"] == 1)
    pz_helper = (me["pz"] == 0, me["pz"] == 3)

    def px_start(step, side):
        @pl.when(there("px", side))
        def _():
            px_copy(step, side).start()

    def px_arrived(step, side):
        @pl.when(there("px", side))
        def _():
            px_copy(step, 1 - side, peer("px", side)).wait_recv()

    def px_sent(step, side):
        @pl.when(there("px", side))
        def _():
            px_copy(step, side).wait_send()

    def pz_start(step, k):
        for side in (0, 1):
            via = jnp.logical_and(pz_sender[side], half(k))

            @pl.when(jnp.logical_and(there("pz", side), jnp.logical_not(via)))
            def _():
                pz_copy(step, side, k).start()

            @pl.when(via)
            def _():
                pz_via_copy(step, side, k).start()

    def pz_pass(step, k):
        for q in (0, 1):
            @pl.when(jnp.logical_and(pz_helper[q], half(k)))
            def _():
                pz_via_copy(step, q, k).wait_recv()
                pz_on_copy(step, q, k).start()

    def goes_via(q, k):
        return jnp.logical_and(jnp.logical_and(parity[q], there("py", q)), share(mine[q], k))

    def held(q, k):
        return jnp.logical_and(parity[q], share(others[q], k))

    def send_early(step, k):
        for q in (0, 1):
            @pl.when(goes_via(q, k))
            def _():
                via_copy(step, q, k).start()

    def send(step, k):
        for q in (0, 1):
            @pl.when(jnp.logical_and(there("py", q), jnp.logical_not(goes_via(q, k))))
            def _():
                py_copy(step, q, k).start()

            @pl.when(held(q, k))
            def _():
                via_copy(step, q, k).wait_recv()
                on_copy(step, q, k).start()

    def sent(step, k):
        for q in (0, 1):
            @pl.when(there("py", q))
            def _():
                py_copy(step, q, k).wait_send()

            @pl.when(there("pz", q))
            def _():
                pz_copy(step, q, k).wait_send()

            @pl.when(jnp.logical_and(pz_helper[q], half(k)))
            def _():
                pz_on_copy(step, q, k).wait_send()

            @pl.when(held(q, k))
            def _():
                on_copy(step, q, k).wait_send()

    loop(chunks, lambda k: send_early(0, k))
    loop(EARLY, lambda k: send(0, k))
    for side in (0, 1):
        px_start(0, side)

    for side in (0, 1):
        @pl.when(jnp.logical_not(there("px", side)))
        def _():
            for slot in bufs:
                for p in range(planes):
                    slot[p, 0 if side == 0 else rows + 1] = jnp.zeros(slot.shape[2:], slot.dtype)

        @pl.when(jnp.logical_not(there("pz", side)))
        def _():
            for step in range(STEPS):
                for k in range(chunks):
                    pz_in[step, side, k] = jnp.zeros(pz_in.shape[3:], pz_in.dtype)

    loads[0].wait()

    def pack(k):
        for i in range(ROWS):
            for p in range(planes):
                pz_out[0, 0, k, p * ROWS + i:p * ROWS + i + 1] = buf0[p, k * ROWS + i + 1, 0:1]
                pz_out[0, 1, k, p * ROWS + i:p * ROWS + i + 1] = buf0[p, k * ROWS + i + 1, cols - 1:cols]
        pz_start(0, k)
    loop(chunks, pack)
    loop(AHEAD, lambda k: pz_pass(0, k))
    loop(AHEAD, lambda k: send(0, k), EARLY)
    loads[1].wait()

    inside = [there("py", side) for side in (0, 1)]

    for step in range(STEPS):
        now, later = bufs[step % 2], bufs[(step + 1) % 2]

        def update(k, which):
            def row(i):
                r = k * ROWS + i
                for p in which:
                    mid = now[p, r + 1]
                    lower = jnp.where(inside[0], halo[step, 0, r], 0.0) if p == 0 else now[p - 1, r + 1]
                    upper = jnp.where(inside[1], halo[step, 1, r], 0.0) if p == planes - 1 else now[p + 1, r + 1]
                    left = jnp.concatenate([pz_in[step, 0, k, pl.ds(p * ROWS + i, 1)], mid[:-1]], axis=0)
                    right = jnp.concatenate([mid[1:], pz_in[step, 1, k, pl.ds(p * ROWS + i, 1)]], axis=0)
                    spread = lower + upper + now[p, r] + now[p, r + 2] + left + right - 6.0 * mid
                    new = mid + 0.1 * spread + 0.2 * mid * (1.0 - mid * inv[p, r])
                    later[p, r + 1] = new
                    if step < STEPS - 1:
                        pz_out[step + 1, 0, k, pl.ds(p * ROWS + i, 1)] = new[0:1]
                        pz_out[step + 1, 1, k, pl.ds(p * ROWS + i, 1)] = new[cols - 1:cols]
            loop(ROWS, row)

        def chunk(k):
            for side in (0, 1):
                @pl.when(there("pz", side))
                def _():
                    pz_copy(step, 1 - side, k, peer("pz", side)).wait_recv()
            if step >= 1:
                sent(step - 1, k)
            update(k, range(1, planes - 1))
            for side in (0, 1):
                @pl.when(there("py", side))
                def _():
                    py_copy(step, 1 - side, k, peer("py", side)).wait_recv()
            update(k, (0, planes - 1))
            if step < STEPS - 1:
                send_early(step + 1, k)
                pz_start(step + 1, k)

        def first(k):
            pz_pass(step, k + AHEAD)
            send(step, k + AHEAD)
            chunk(k)

        def second(k):
            chunk(k)
            if step < STEPS - 1:
                pz_pass(step + 1, k - (chunks - AHEAD))
                send(step + 1, k - (chunks - AHEAD))

        px_arrived(step, 0)
        loop(chunks - AHEAD, first)
        if step < STEPS - 1:
            px_start(step + 1, 0)
        px_arrived(step, 1)
        for side in (0, 1):
            px_sent(step, side)
        loop(chunks, second, chunks - AHEAD)
        if step < STEPS - 1:
            px_start(step + 1, 1)

    loop(chunks, lambda k: sent(STEPS - 1, k))


def drain(held_ref, out_ref, sem):
    rows = out_ref.shape[1]
    copies = [
        pltpu.make_async_copy(held_ref.at[p, pl.ds(1, rows)], out_ref.at[p], sem.at[p])
        for p in range(out_ref.shape[0])
    ]
    for copy in copies:
        copy.start()
    for copy in copies:
        copy.wait()


def local(sizes, u, inv):
    planes, rows, cols, levels = u.shape
    chunks = rows // ROWS
    dma = pltpu.SemaphoreType.DMA
    held, _ = pl.pallas_call(
        functools.partial(kernel, sizes),
        out_shape=(pltpu.VMEM((planes, rows + 2, cols, levels), u.dtype),
                   jax.ShapeDtypeStruct((STEPS, chunks, ROWS, cols, levels), u.dtype)),
        in_specs=[pl.BlockSpec(memory_space=pl.ANY)] * 2,
        out_specs=(pl.BlockSpec(memory_space=pltpu.VMEM), pl.BlockSpec(memory_space=pl.ANY)),
        scratch_shapes=[
            pltpu.VMEM((planes, rows + 2, cols, levels), u.dtype),
            pltpu.VMEM(u.shape, u.dtype),
            pltpu.VMEM((STEPS, 2, rows, cols, levels), u.dtype),
            pltpu.VMEM((STEPS, 2, chunks, planes * ROWS, levels), u.dtype),
            pltpu.VMEM((STEPS, 2, chunks, planes * ROWS, levels), u.dtype),
            dma((2,)),
            dma((STEPS, 2, chunks)),
            dma((STEPS, 2, chunks)),
            dma((STEPS, 2)),
            dma((STEPS, 2)),
            dma((STEPS, 2, chunks)),
            dma((STEPS, 2, chunks)),
            dma((STEPS, chunks)),
            dma((STEPS, chunks)),
            pltpu.VMEM((STEPS, chunks, planes * ROWS, levels), u.dtype),
            dma((STEPS, chunks)),
            dma((STEPS, chunks)),
        ],
        compiler_params=pltpu.CompilerParams(
            collective_id=0, has_side_effects=True, vmem_limit_bytes=48 * 2**20),
    )(u, inv)
    return pl.pallas_call(
        drain,
        out_shape=jax.ShapeDtypeStruct(u.shape, u.dtype),
        in_specs=[pl.BlockSpec(memory_space=pltpu.VMEM)],
        out_specs=pl.BlockSpec(memory_space=pl.ANY),
        scratch_shapes=[dma((planes,))],
        compiler_params=pltpu.CompilerParams(vmem_limit_bytes=2**20),
    )(held)


def solution(mesh):
    spec = P("py", "px", "pz", None)
    sizes = {axis: mesh.shape[axis] for axis in ("py", "px", "pz")}
    return jax.shard_map(functools.partial(local, sizes), mesh=mesh, in_specs=(spec, spec),
                         out_specs=spec, check_vma=False)
```

time: 406 us -> 390 us (0.961)
  local copies, waits for them, and re-layouts: 10.6 us -> 0 us
    unnamed x1 -> x0, local copies, waits for them, and re-layouts: 10.6 us -> none
    pallas_call x1 -> x2, Pallas kernels: 392 us -> 390 us  [the longest x1 385 us: local(): pl.pallas_call(functools.partial(kernel, sizes), out_shape=(pltpu.VMEM((p...]
where the time goes in v3:
time: 390 us
  Pallas kernels  390 us (100%)
    pallas_call x1, Pallas kernels, local(): pl.pallas_call(functools.partial(kernel, sizes), out_shape=(pltpu.VMEM((p...  385 us

profile of v3, /device:TPU:7, one launch (start us, length us, event | category | flops | bytes accessed | tf_op | source)
XLA Modules:
  0.0 390.1 jit_solution(4270003800719059106)
XLA Ops:
  0.0 385.3 %shard_map.28 = (f32[4,66,96,128]{3,2,1,0:T(8,128)S(1)}, f32[3,16,4,96,128]{4,3,2,1,0:T(8,128)}) custom-call(f32[4,64,96,128]{3,2,1,0:T(8,128)} %u_ref.1, f32[4,64,96,128]{3,2,1,0:T(8,128)} %inv_ref.1), custom_call_target="tpu_custom_call" | custom-call | tf_op jit(solution)/shard_map/pallas_call | solution.py:316
  385.3 4.7 %shard_map.29 = f32[4,64,96,128]{3,2,1,0:T(8,128)} custom-call(f32[4,66,96,128]{3,2,1,0:T(8,128)S(1)} %get-tuple-element.6.held_ref), custom_call_target="tpu_custom_call" | custom-call | tf_op jit(solution)/shard_map/pallas_call | solution.py:344

commit v4 on v3

--- a/solution.py
+++ b/solution.py
@@ -8,14 +8,14 @@
 from jax.sharding import PartitionSpec as P
 
 STEPS = 3
-ROWS = 4
-AHEAD = 8
+ROWS = 8
+AHEAD = 4
 EARLY = 2
 MESH = pl.DeviceIdType.MESH
 
 
 def share(n, k):
-    return k % 4 < n
+    return k % 4 >= 4 - n
 
 
 def half(k):

time: 390 us -> 383 us (0.982)
  Pallas kernels: 390 us -> 383 us
    pallas_call x1, Pallas kernels: 385 us -> 379 us  [local(): pl.pallas_call(functools.partial(kernel, sizes), out_shape=(pltpu.VMEM((p...]
where the time goes in v4:
time: 383 us
  Pallas kernels  383 us (100%)
    pallas_call x1, Pallas kernels, local(): pl.pallas_call(functools.partial(kernel, sizes), out_shape=(pltpu.VMEM((p...  379 us

profile of v4, /device:TPU:7, one launch (start us, length us, event | category | flops | bytes accessed | tf_op | source)
XLA Modules:
  0.0 383.3 jit_solution(3498415760667342851)
XLA Ops:
  0.0 378.6 %shard_map.28 = (f32[4,66,96,128]{3,2,1,0:T(8,128)S(1)}, f32[3,8,8,96,128]{4,3,2,1,0:T(8,128)}) custom-call(f32[4,64,96,128]{3,2,1,0:T(8,128)} %u_ref.1, f32[4,64,96,128]{3,2,1,0:T(8,128)} %inv_ref.1), custom_call_target="tpu_custom_call" | custom-call | tf_op jit(solution)/shard_map/pallas_call | solution.py:316
  378.6 4.7 %shard_map.29 = f32[4,64,96,128]{3,2,1,0:T(8,128)} custom-call(f32[4,66,96,128]{3,2,1,0:T(8,128)S(1)} %get-tuple-element.6.held_ref), custom_call_target="tpu_custom_call" | custom-call | tf_op jit(solution)/shard_map/pallas_call | solution.py:344

commit v5 on v4

--- a/solution.py
+++ b/solution.py
@@ -8,9 +8,9 @@
 from jax.sharding import PartitionSpec as P
 
 STEPS = 3
-ROWS = 8
-AHEAD = 4
-EARLY = 2
+ROWS = 16
+AHEAD = 2
+EARLY = 1
 MESH = pl.DeviceIdType.MESH
 
 
@@ -85,11 +85,11 @@
             send_sem=py_send.at[step, side, k], recv_sem=py_recv.at[step, 1 - side, k],
             device_id=peer("py", side) if device is None else device, device_id_type=MESH)
 
-    def via_copy(step, q, k):
+    def via_copy(step, q, k, towards=1):
         return pltpu.make_async_remote_copy(
             src_ref=source(step, q, k), dst_ref=transit.at[step, k],
             send_sem=py_send.at[step, q, k], recv_sem=via_recv.at[step, k],
-            device_id={"py": me["py"] + (2 if q else -2)}, device_id_type=MESH)
+            device_id={"py": me["py"] + towards * (2 if q else -2)}, device_id_type=MESH)
 
     def on_copy(step, q, k):
         at = pl.multiple_of(k * ROWS, ROWS)
@@ -112,11 +112,11 @@
             send_sem=pz_send.at[step, side, k], recv_sem=pz_recv.at[step, 1 - side, k],
             device_id=peer("pz", side) if device is None else device, device_id_type=MESH)
 
-    def pz_via_copy(step, q, k):
+    def pz_via_copy(step, q, k, towards=1):
         return pltpu.make_async_remote_copy(
             src_ref=pz_out.at[step, q, k], dst_ref=pz_transit.at[step, k],
             send_sem=pz_send.at[step, q, k], recv_sem=pz_via_recv.at[step, k],
-            device_id={"pz": me["pz"] + (2 if q else -2)}, device_id_type=MESH)
+            device_id={"pz": me["pz"] + towards * (2 if q else -2)}, device_id_type=MESH)
 
     def pz_on_copy(step, q, k):
         return pltpu.make_async_remote_copy(
@@ -158,7 +158,7 @@
         for q in (0, 1):
             @pl.when(jnp.logical_and(pz_helper[q], half(k)))
             def _():
-                pz_via_copy(step, q, k).wait_recv()
+                pz_via_copy(step, q, k, -1).wait_recv()
                 pz_on_copy(step, q, k).start()
 
     def goes_via(q, k):
@@ -181,7 +181,7 @@
 
             @pl.when(held(q, k))
             def _():
-                via_copy(step, q, k).wait_recv()
+                via_copy(step, q, k, -1).wait_recv()
                 on_copy(step, q, k).start()
 
     def sent(step, k):
@@ -238,13 +238,28 @@
     for step in range(STEPS):
         now, later = bufs[step % 2], bufs[(step + 1) % 2]
 
+        final = step == STEPS - 1
+
+        def beyond(side, r):
+            return jnp.where(inside[side], halo[step, side, r], 0.0)
+
+        def outside(side, r):
+            return jnp.zeros(halo.shape[3:], halo.dtype) if final else beyond(side, r)
+
+        def complete(k):
+            def row(i):
+                r = k * ROWS + i
+                for side, p in enumerate((0, planes - 1)):
+                    later[p, r + 1] += 0.1 * beyond(side, r)
+            loop(ROWS, row)
+
         def update(k, which):
             def row(i):
                 r = k * ROWS + i
                 for p in which:
                     mid = now[p, r + 1]
-                    lower = jnp.where(inside[0], halo[step, 0, r], 0.0) if p == 0 else now[p - 1, r + 1]
-                    upper = jnp.where(inside[1], halo[step, 1, r], 0.0) if p == planes - 1 else now[p + 1, r + 1]
+                    lower = outside(0, r) if p == 0 else now[p - 1, r + 1]
+                    upper = outside(1, r) if p == planes - 1 else now[p + 1, r + 1]
                     left = jnp.concatenate([pz_in[step, 0, k, pl.ds(p * ROWS + i, 1)], mid[:-1]], axis=0)
                     right = jnp.concatenate([mid[1:], pz_in[step, 1, k, pl.ds(p * ROWS + i, 1)]], axis=0)
                     spread = lower + upper + now[p, r] + now[p, r + 2] + left + right - 6.0 * mid
@@ -262,12 +277,15 @@
                     pz_copy(step, 1 - side, k, peer("pz", side)).wait_recv()
             if step >= 1:
                 sent(step - 1, k)
-            update(k, range(1, planes - 1))
+            update(k, range(planes) if final else range(1, planes - 1))
             for side in (0, 1):
                 @pl.when(there("py", side))
                 def _():
                     py_copy(step, 1 - side, k, peer("py", side)).wait_recv()
-            update(k, (0, planes - 1))
+            if final:
+                complete(k)
+            else:
+                update(k, (0, planes - 1))
             if step < STEPS - 1:
                 send_early(step + 1, k)
                 pz_start(step + 1, k)

time: 383 us -> 381 us (level)
  Pallas kernels: 383 us -> 378 us
    pallas_call x1, Pallas kernels: 379 us -> 374 us  [local(): pl.pallas_call(functools.partial(kernel, sizes), out_shape=(pltpu.VMEM((p...]
where the time goes in v5:
time: 381 us; the launch traced here: 378 us
  Pallas kernels  378 us (99%)
    pallas_call x1, Pallas kernels, local(): pl.pallas_call(functools.partial(kernel, sizes), out_shape=(pltpu.VMEM((p...  374 us

profile of v5, /device:TPU:7, one launch (start us, length us, event | category | flops | bytes accessed | tf_op | source)
XLA Modules:
  0.0 378.4 jit_solution(2660065202267443328)
XLA Ops:
  0.0 373.7 %shard_map.28 = (f32[4,66,96,128]{3,2,1,0:T(8,128)S(1)}, f32[3,4,16,96,128]{4,3,2,1,0:T(8,128)}) custom-call(f32[4,64,96,128]{3,2,1,0:T(8,128)} %u_ref.1, f32[4,64,96,128]{3,2,1,0:T(8,128)} %inv_ref.1), custom_call_target="tpu_custom_call" | custom-call | tf_op jit(solution)/shard_map/pallas_call | solution.py:334
  373.7 4.7 %shard_map.29 = f32[4,64,96,128]{3,2,1,0:T(8,128)} custom-call(f32[4,66,96,128]{3,2,1,0:T(8,128)S(1)} %get-tuple-element.6.held_ref), custom_call_target="tpu_custom_call" | custom-call | tf_op jit(solution)/shard_map/pallas_call | solution.py:362

commit v6 on v5

--- a/solution.py
+++ b/solution.py
@@ -18,8 +18,12 @@
     return k % 4 >= 4 - n
 
 
+def opens(k):
+    return k % 2 == 0
+
+
 def half(k):
-    return k % 2 == 1
+    return k % 4 == 0
 
 
 def kernel(sizes, u_ref, inv_ref, out_ref, transit, buf0, inv, halo, pz_in, pz_out,
@@ -50,8 +54,6 @@
         pltpu.make_async_copy(u_ref, buf0.at[:, pl.ds(1, rows)], load_sem.at[0]),
         pltpu.make_async_copy(inv_ref, inv, load_sem.at[1]),
     ]
-    for load in loads:
-        load.start()
 
     barrier = pltpu.get_barrier_semaphore()
     peers = jnp.int32(0)
@@ -108,19 +110,19 @@
 
     def pz_copy(step, side, k, device=None):
         return pltpu.make_async_remote_copy(
-            src_ref=pz_out.at[step, side, k], dst_ref=pz_in.at[step, 1 - side, k],
+            src_ref=pz_out.at[step, side, pl.ds(k, 2)], dst_ref=pz_in.at[step, 1 - side, pl.ds(k, 2)],
             send_sem=pz_send.at[step, side, k], recv_sem=pz_recv.at[step, 1 - side, k],
             device_id=peer("pz", side) if device is None else device, device_id_type=MESH)
 
     def pz_via_copy(step, q, k, towards=1):
         return pltpu.make_async_remote_copy(
-            src_ref=pz_out.at[step, q, k], dst_ref=pz_transit.at[step, k],
+            src_ref=pz_out.at[step, q, pl.ds(k, 2)], dst_ref=pz_transit.at[step, pl.ds(k, 2)],
             send_sem=pz_send.at[step, q, k], recv_sem=pz_via_recv.at[step, k],
             device_id={"pz": me["pz"] + towards * (2 if q else -2)}, device_id_type=MESH)
 
     def pz_on_copy(step, q, k):
         return pltpu.make_async_remote_copy(
-            src_ref=pz_transit.at[step, k], dst_ref=pz_in.at[step, 1 - q, k],
+            src_ref=pz_transit.at[step, pl.ds(k, 2)], dst_ref=pz_in.at[step, 1 - q, pl.ds(k, 2)],
             send_sem=pz_via_send.at[step, k], recv_sem=pz_recv.at[step, 1 - q, k],
             device_id=peer("pz", 1 - q), device_id_type=MESH)
 
@@ -190,7 +192,7 @@
             def _():
                 py_copy(step, q, k).wait_send()
 
-            @pl.when(there("pz", q))
+            @pl.when(jnp.logical_and(there("pz", q), opens(k)))
             def _():
                 pz_copy(step, q, k).wait_send()
 
@@ -204,8 +206,10 @@
 
     loop(chunks, lambda k: send_early(0, k))
     loop(EARLY, lambda k: send(0, k))
+    loads[0].start()
     for side in (0, 1):
         px_start(0, side)
+    loads[1].start()
 
     for side in (0, 1):
         @pl.when(jnp.logical_not(there("px", side)))
@@ -227,7 +231,10 @@
             for p in range(planes):
                 pz_out[0, 0, k, p * ROWS + i:p * ROWS + i + 1] = buf0[p, k * ROWS + i + 1, 0:1]
                 pz_out[0, 1, k, p * ROWS + i:p * ROWS + i + 1] = buf0[p, k * ROWS + i + 1, cols - 1:cols]
-        pz_start(0, k)
+
+        @pl.when(jnp.logical_not(opens(k)))
+        def _():
+            pz_start(0, k - 1)
     loop(chunks, pack)
     loop(AHEAD, lambda k: pz_pass(0, k))
     loop(AHEAD, lambda k: send(0, k), EARLY)
@@ -272,7 +279,7 @@
 
         def chunk(k):
             for side in (0, 1):
-                @pl.when(there("pz", side))
+                @pl.when(jnp.logical_and(there("pz", side), opens(k)))
                 def _():
                     pz_copy(step, 1 - side, k, peer("pz", side)).wait_recv()
             if step >= 1:
@@ -288,7 +295,10 @@
                 update(k, (0, planes - 1))
             if step < STEPS - 1:
                 send_early(step + 1, k)
-                pz_start(step + 1, k)
+
+                @pl.when(jnp.logical_not(opens(k)))
+                def _():
+                    pz_start(step + 1, k - 1)
 
         def first(k):
             pz_pass(step, k + AHEAD)

time: 381 us -> 381 us (level)
  no operation moved by 1% of the time
where the time goes in v6:
time: 381 us; the launch traced here: 378 us
  Pallas kernels  378 us (99%)
    pallas_call x1, Pallas kernels, local(): pl.pallas_call(functools.partial(kernel, sizes), out_shape=(pltpu.VMEM((p...  374 us

profile of v6, /device:TPU:7, one launch (start us, length us, event | category | flops | bytes accessed | tf_op | source)
XLA Modules:
  0.0 378.4 jit_solution(809522103678637573)
XLA Ops:
  0.0 373.7 %shard_map.28 = (f32[4,66,96,128]{3,2,1,0:T(8,128)S(1)}, f32[3,4,16,96,128]{4,3,2,1,0:T(8,128)}) custom-call(f32[4,64,96,128]{3,2,1,0:T(8,128)} %u_ref.1, f32[4,64,96,128]{3,2,1,0:T(8,128)} %inv_ref.1), custom_call_target="tpu_custom_call" | custom-call | tf_op jit(solution)/shard_map/pallas_call | solution.py:344
  373.7 4.7 %shard_map.29 = f32[4,64,96,128]{3,2,1,0:T(8,128)} custom-call(f32[4,66,96,128]{3,2,1,0:T(8,128)S(1)} %get-tuple-element.6.held_ref), custom_call_target="tpu_custom_call" | custom-call | tf_op jit(solution)/shard_map/pallas_call | solution.py:372

commit v7 on v6

--- a/solution.py
+++ b/solution.py
@@ -177,7 +177,12 @@
 
     def send(step, k):
         for q in (0, 1):
-            @pl.when(jnp.logical_and(there("py", q), jnp.logical_not(goes_via(q, k))))
+            @pl.when(jnp.logical_and(parity[1 - q], there("py", q)))
+            def _():
+                py_copy(step, q, k).start()
+
+        for q in (0, 1):
+            @pl.when(jnp.logical_and(jnp.logical_and(parity[q], there("py", q)), jnp.logical_not(goes_via(q, k))))
             def _():
                 py_copy(step, q, k).start()
 

time: 381 us -> 381 us (level)
  no operation moved by 1% of the time
where the time goes in v7:
time: 381 us; the launch traced here: 378 us
  Pallas kernels  378 us (99%)
    pallas_call x1, Pallas kernels, local(): pl.pallas_call(functools.partial(kernel, sizes), out_shape=(pltpu.VMEM((p...  374 us

profile of v7, /device:TPU:7, one launch (start us, length us, event | category | flops | bytes accessed | tf_op | source)
XLA Modules:
  0.0 378.4 jit_solution(8226768663515724046)
XLA Ops:
  0.0 373.7 %shard_map.28 = (f32[4,66,96,128]{3,2,1,0:T(8,128)S(1)}, f32[3,4,16,96,128]{4,3,2,1,0:T(8,128)}) custom-call(f32[4,64,96,128]{3,2,1,0:T(8,128)} %u_ref.1, f32[4,64,96,128]{3,2,1,0:T(8,128)} %inv_ref.1), custom_call_target="tpu_custom_call" | custom-call | tf_op jit(solution)/shard_map/pallas_call | solution.py:349
  373.7 4.7 %shard_map.29 = f32[4,64,96,128]{3,2,1,0:T(8,128)} custom-call(f32[4,66,96,128]{3,2,1,0:T(8,128)S(1)} %get-tuple-element.6.held_ref), custom_call_target="tpu_custom_call" | custom-call | tf_op jit(solution)/shard_map/pallas_call | solution.py:377
